TPU v7x, 32 devices: a whole 2x2x4 slice. The times are simulated.
32 devices in a mesh: row: 8 (over y, x, core), col: 4 (over z).
Axes of the slice: x: 2, y: 2, z: 4, core: 2. Of those that a mesh axis runs over, the one named last changes fastest.
Arguments:
- acts: bfloat16 [512, 16384], P('row', 'col'), may hold values from -6 to 6
- grads: float32 [16384, 512], P('col', 'row'), may hold values from -24 to 24
Outputs:
- factor: float32 [16384, 16384], P('row', 'col')
- applied: float32 [16384, 512], P('row', 'col')
- solution: float32 [16384, 512], P('col', 'row')
All inputs are finite; a program needn't handle non-finite values.
Results may differ from a plain program's by a relative error of at most 0.0003.
Values may be sent and summed in bfloat16 or wider, within the bound.
No kernel may reach another device: no remote copies, remote signals or barrier semaphores. Data moves between devices by JAX's collectives and lax.ppermute only.
A program may use at most 128 MiB of HBM per device.

v0:
```python
import math

import jax
import jax.numpy as jnp
from jax import lax
from jax.sharding import PartitionSpec as P

damping = 1.0
highest = lax.Precision.HIGHEST


def from_root(value, axis, source):
    kept = jnp.where(lax.axis_index(axis) == source, value, 0).astype(value.dtype)
    return lax.psum(kept, axis)


def step_size(feature_count, token_count):
    return 1.0 / (damping + (1.0 + math.sqrt(feature_count / token_count)) ** 2)


def local(acts, grads):
    row_count = lax.axis_size("row")
    col_count = lax.axis_size("col")
    row_ratio = row_count // col_count
    row_index = lax.axis_index("row")
    col_index = lax.axis_index("col")
    outer_width = acts.shape[1]
    inner_width = outer_width // row_ratio
    token_count = acts.shape[0] * row_count
    omega_step = step_size(outer_width * col_count, token_count)
    row_offset = row_index % row_ratio * inner_width
    owner_col = row_index // row_ratio
    column_panel = lax.all_gather(acts, "row", axis=0, tiled=True)
    owned_slice = lax.dynamic_slice_in_dim(column_panel, row_offset, inner_width, 1)
    inner_panel = from_root(owned_slice, "col", owner_col)
    gram_sum = lax.dot_general(
        inner_panel, column_panel, (((0,), (0,)), ((), ())), preferred_element_type=jnp.float32
    )
    gram_tile = gram_sum / token_count
    is_owner = (col_index == owner_col).astype(jnp.float32)
    gathered = lax.all_gather(grads, "row", axis=1, tiled=True)
    mirror_rows = lax.dynamic_slice_in_dim(gathered, row_offset, inner_width, 0)
    partial_sum = jnp.dot(gram_tile, gathered, precision=highest) + damping * is_owner * mirror_rows
    full_applied = lax.psum(partial_sum, "col")
    share = full_applied.shape[1] // col_count
    applied = lax.dynamic_slice_in_dim(full_applied, col_index * share, share, 1)
    mirror_coef = omega_step**3 * damping - 3.0 * omega_step**2
    empty_block = jnp.zeros((outer_width, full_applied.shape[1]), jnp.float32)
    placed = lax.dynamic_update_slice_in_dim(
        empty_block, full_applied * (mirror_coef * is_owner), row_offset, 0
    )
    second_sum = (
        omega_step**3
        * lax.dot_general(
            gram_tile,
            full_applied,
            (((0,), (0,)), ((), ())),
            precision=highest,
            preferred_element_type=jnp.float32,
        )
        + placed
    )
    solution = 3.0 * omega_step * grads + lax.psum_scatter(
        second_sum, "row", scatter_dimension=1, tiled=True
    )
    return (gram_tile, applied, solution)


def solution(mesh):
    in_specs = (P("row", "col"), P("col", "row"))
    out_specs = (P("row", "col"), P("row", "col"), P("col", "row"))
    return jax.shard_map(local, mesh=mesh, in_specs=in_specs, out_specs=out_specs, check_vma=False)
```

profile of v0, /device:TPU:0, one launch (start us, length us, event | category | flops | bytes accessed | tf_op | source)
XLA Modules:
  0.0 583.2 jit_solution(10916674862800319205)
XLA Ops:
  7.2 0.0 all-gather.3.cloned.1.call-start
  7.2 0.7 all-gather.3.cloned.1.call-update
  7.9 0.0 all-reduce.3.cloned.1.call-start
  8.0 41.2 %all-gather.3.cloned.1.call-done = bf16[512,4096]{1,0:T(8,128)(2,1)} async-done(((bf16[64,4096]{1,0:T(8,128)(2,1)}), bf16[512,4096]{1,0:T(8,128)(2,1)}) %all-gather.3.cloned.1.call-update) | async-done | bytes 4194320 | tf_op jit(solution)/shard_map/all_gather | solution.py:33
  49.2 3.4 dynamic-slice_select_fusion
  52.6 0.0 all-reduce.3.cloned.1.call-update
  52.7 0.0 all-gather.5.cloned.1.call-start
  52.7 0.7 all-gather.5.cloned.1.call-update
  53.4 0.0 all-reduce.5.cloned.1.call-start
  53.5 85.5 %all-reduce.3.cloned.1.call-done = bf16[512,2048]{1,0:T(8,128)(2,1)} async-done(((bf16[512,2048]{1,0:T(8,128)(2,1)}), bf16[512,2048]{1,0:T(8,128)(2,1)}) %all-reduce.3.cloned.1.call-update) | async-done | bytes 2097168 | tf_op jit(solution)/shard_map/psum | solution.py:14
  139.0 18.8 %convolution_multiply_fusion = f32[2048,4096]{1,0:T(8,128)} fusion(bf16[512,2048]{1,0:T(8,128)(2,1)} %all-reduce.3.cloned.1.call-done, bf16[512,4096]{1,0:T(8,128)(2,1)} %all-gather.3.cloned.1.call-done), kind=kOutput, calls=%fused_computation | convolution fusion | flops 8598323200 | bytes 39845888 | tf_op jit(solution)/shard_map/dot_general | solution.py:36
  157.7 36.5 %all-gather.5.cloned.1.call-done = f32[4096,512]{0,1:T(8,128)} async-done(((f32[4096,64]{0,1:T(8,128)}), f32[4096,512]{0,1:T(8,128)}) %all-gather.5.cloned.1.call-update) | async-done | bytes 8388624 | tf_op jit(solution)/shard_map/all_gather | solution.py:41
  194.2 4.6 constant_dynamic-slice_fusion.1
  198.8 5.3 copy.13
  204.2 62.2 %multiply_add_fusion = f32[2048,512]{1,0:T(8,128)} fusion(f32[2048,512]{1,0:T(8,128)} %copy.13, f32[2048,4096]{1,0:T(8,128)} %convolution_multiply_fusion, f32[4096,512]{0,1:T(8,128)} %all-gather.5.cloned.1.call-done, f32[]{:T(128)S(6)} %convert_element_type.5), kind=kOutput, calls=%fused_computation.3 | convolution fusion | flops 51541704704 | bytes 50331652 | tf_op jit(solution)/shard_map/dot_general | solution.py:43
  266.3 0.0 all-reduce.5.cloned.1.call-update
  266.4 0.0 reduce-scatter.4.cloned.1.call-start
  266.4 155.1 %all-reduce.5.cloned.1.call-done = f32[2048,512]{1,0:T(8,128)} async-done(((f32[2048,512]{1,0:T(8,128)}), f32[2048,512]{1,0:T(8,128)}) %all-reduce.5.cloned.1.call-update) | async-done | bytes 4194320 | tf_op jit(solution)/shard_map/psum | solution.py:44
  421.5 0.0 copy-start
  421.5 60.8 %convolution_multiply_fusion.1 = f32[4096,512]{1,0:T(8,128)} fusion(f32[2048,4096]{1,0:T(8,128)} %convolution_multiply_fusion, f32[2048,512]{1,0:T(8,128)} %all-reduce.5.cloned.1.call-done), kind=kOutput, calls=%fused_computation.1 | convolution fusion | flops 51541704704 | bytes 46137344 | tf_op jit(solution)/shard_map/dot_general | solution.py:54
  482.3 0.0 copy-done
  482.3 5.2 add_dynamic-update-slice_fusion
  487.5 9.0 %copy.11 = f32[4096,512]{0,1:T(8,128)} copy(f32[4096,512]{1,0:T(8,128)} %add_dynamic-update-slice_fusion) | data formatting | bytes 16777216
  496.5 0.0 copy-start.1
  496.5 0.0 reduce-scatter.4.cloned.1.call-update
  496.5 1.2 copy-done.1
  497.7 0.6 copy.9
  498.3 2.3 constant_dynamic-slice_fusion
  500.6 66.6 %reduce-scatter.4.cloned.1.call-done = f32[64,4096]{1,0:T(8,128)} async-done(((f32[512,4096]{1,0:T(8,128)}), f32[64,4096]{1,0:T(8,128)}) %reduce-scatter.4.cloned.1.call-update) | async-done | bytes 1048592
  567.2 3.2 copy.12
  570.4 3.2 multiply_add_fusion.1
  573.5 3.1 copy.10
Async XLA Ops:
  7.2 42.0 %all-gather.3.cloned.1.call-start = ((), (), s32[]{:S(2)}) async-start(), calls=%async_computation.1 | async-start | bytes 4718592 | tf_op jit(solution)/shard_map/all_gather | solution.py:33
  7.9 131.1 %all-reduce.3.cloned.1.call-start = ((), (), s32[]{:S(2)}) async-start(), calls=%async_computation.2 | async-start | bytes 4194304 | tf_op jit(solution)/shard_map/psum | solution.py:14
  52.7 141.5 %all-gather.5.cloned.1.call-start = ((), (), s32[]{:S(2)}) async-start(), calls=%async_computation.3 | async-start | bytes 9437184 | tf_op jit(solution)/shard_map/all_gather | solution.py:41
  53.4 368.1 %all-reduce.5.cloned.1.call-start = ((), (), s32[]{:S(2)}) async-start(), calls=%async_computation.4 | async-start | bytes 8388608 | tf_op jit(solution)/shard_map/psum | solution.py:44
  266.4 300.8 %reduce-scatter.4.cloned.1.call-start = ((), (), s32[]{:S(2)}) async-start(), calls=%async_computation.5 | async-start | bytes 9437184
  421.5 60.8 %copy-start = (f32[2048,512]{1,0:T(8,128)S(1)}, f32[2048,512]{1,0:T(8,128)}, u32[]{:S(2)}) copy-start(f32[2048,512]{1,0:T(8,128)} %all-reduce.5.cloned.1.call-done) | copy-start | bytes 12582916
  496.5 1.2 copy-start.1
Sparse Core Ops, SparseCore 0:
  9.9 39.2 all-gather.2
  52.8 86.1 all-reduce.2
  140.9 53.2 all-gather.4
  266.5 154.9 all-reduce.4
  496.7 70.4 reduce-scatter.3
where the time goes:
time: 584 us; the launch traced here: 583 us
  waiting for transfers between devices  386 us (66%)
  matrix products  142 us (24%)
  local copies, waits for them, and re-layouts  29.4 us (5%)
  between operations  13.8 us (2%)
  other arithmetic  11.8 us (2%)
    psum x1, waiting for transfers between devices, local(): full_applied = lax.psum(partial_sum, 'col')  155 us
    psum x1, waiting for transfers between devices, from_root(): return lax.psum(kept, axis)  85.5 us
    unnamed x6, waiting for transfers between devices  68 us
    dot_general x1, matrix products, local(): jnp.dot(gram_tile, gathered, precision=highest)  62.2 us
    dot_general x1, matrix products, local(): lax.dot_general(gram_tile, full_applied, (((0,), (0,)), ((), ())), precis...  60.8 us
    all_gather x1, waiting for transfers between devices, local(): column_panel = lax.all_gather(acts, 'row', axis=0, tiled=True)  41.2 us
    all_gather x1, waiting for transfers between devices, local(): gathered = lax.all_gather(grads, 'row', axis=1, tiled=True)  36.5 us
    unnamed x9, local copies, waits for them, and re-layouts  22.5 us
  transfers between devices with their start and end apart: 5, of which 5 were waited for; matrix products, arithmetic and copies ran while one was open for 4% of the time, Pallas kernels for 0%

commit v1 on v0

v1 whole, which is shorter than its diff:
```python
import math

import jax
import jax.numpy as jnp
from jax import lax
from jax.sharding import PartitionSpec as P


damping = 1.0


def step_size(feature_count, token_count):
    return 1.0 / (damping + (1.0 + math.sqrt(feature_count / token_count)) ** 2)


def split(value, axis):
    high = lax.reduce_precision(value, 8, 7)
    low = value - high
    return jnp.concatenate([high.astype(jnp.bfloat16), low.astype(jnp.bfloat16)], axis)


def merge(value):
    half = value.shape[0] // 2
    return value[:half] + value[half:]


def times(left, right, left_dim, right_dim):
    return lax.dot_general(
        left, right, (((left_dim,), (right_dim,)), ((), ())), preferred_element_type=jnp.float32
    )


def middle(z):
    return z in (1, 2)


def plan_inner(layers):
    if layers != 4:
        return [
            {(k, z): (z, k ^ turn) for k in range(layers) for z in range(layers)}
            for turn in range(layers)
        ], []
    flat = [
        {
            (k, z): (k ^ mask, z)
            for k in range(4)
            for z in range(4)
            if middle(z) or k ^ mask in (z, z ^ 1)
        }
        for mask in (1, 2, 3)
    ]
    outer = [
        {
            (k, z): ((2 if z == 1 else 0) + (turn ^ k), 0 if z == 1 else 3)
            for k in range(4)
            for z in (1, 2)
            if turn ^ k in (0, 1)
        }
        for turn in range(4)
    ]
    return flat, outer


def step(acts, grads):
    layers = lax.axis_size("col")
    lanes = lax.axis_size("row") // layers
    row_index = lax.axis_index("row")
    layer = lax.axis_index("col")
    group = row_index // lanes
    lane = row_index % lanes
    tokens, width = acts.shape
    share = width // lanes
    group_tokens = tokens * lanes
    token_count = group_tokens * layers
    omega = step_size(width * layers, token_count)
    bits = [1 << b for b in range(layers.bit_length() - 1)]

    def send(value, rule):
        pairs = []
        for k in range(layers):
            for j in range(lanes):
                for z in range(layers):
                    target = rule(k, j, z)
                    if target is not None:
                        to_k, to_j, to_z = target
                        pairs.append(
                            ((k * lanes + j) * layers + z, (to_k * lanes + to_j) * layers + to_z)
                        )
        return lax.ppermute(value, ("row", "col"), pairs)

    def shift(value, step):
        return send(value, lambda k, j, z: (k, (j + step) % lanes, z))

    def follow(value, plan):
        def rule(k, j, z):
            if (k, z) not in plan:
                return None
            to_k, to_z = plan[k, z]
            return (to_k, j, to_z)

        return send(value, rule)

    def put(whole, part, *spot):
        spot = spot + (0,) * (whole.ndim - len(spot))
        return lax.dynamic_update_slice(whole, part[(None,) * (whole.ndim - part.ndim)], spot)

    grads_t = grads.T

    panel = jnp.broadcast_to(acts, (layers, lanes, tokens, width))
    pieces = {0: acts}
    for mask in range(1, layers):
        pieces[mask] = send(acts, lambda k, j, z: (k ^ mask, j, z))
    swapped = [acts]
    for mask, piece in pieces.items():
        panel = put(panel, piece, group ^ mask, lane)
        for step in range(1, lanes):
            other = shift(piece, step)
            if mask == 0:
                swapped.append(other)
            panel = put(panel, other, group ^ mask, (lane - step) % lanes)
    panel = panel.reshape(token_count, width)

    mine = jnp.broadcast_to(
        lax.dynamic_slice_in_dim(acts, lane * share, share, 1), (lanes, tokens, share)
    )
    for step in range(1, lanes):
        cut = lax.dynamic_slice_in_dim(swapped[step], lane * share, share, 1)
        mine = put(mine, cut, (lane - step) % lanes)
    mine = put(mine, lax.dynamic_slice_in_dim(acts, lane * share, share, 1), lane)
    mine_t = mine.reshape(group_tokens, share).T

    flat, outer = plan_inner(layers)
    if layers == 4:
        held = jnp.broadcast_to(mine_t, (layers, share, group_tokens))
        ways = [
            ({0: 2, 3: 1}, (layer + 2) % 4),
            ({1: 2, 2: 1}, 3 - layer),
            ({0: 1, 1: 0, 2: 3, 3: 2}, layer ^ 1),
        ]
        for goes, spot in ways:
            part = send(mine_t, lambda k, j, z: (k, j, goes[z]) if z in goes else None)
            held = put(held, part, spot)
        held = put(held, mine_t, layer)

        def pick(index):
            return lax.dynamic_index_in_dim(held, index, 0, keepdims=False)

        inner_t = jnp.broadcast_to(pick(group), held.shape)
        for mask, plan in enumerate(flat, 1):
            inner_t = put(inner_t, follow(pick(group ^ mask), plan), group ^ mask)
        first = jnp.where(layer == 1, 2, 0)
        turned = [
            follow(pick(first + ((turn ^ group) & 1)), plan)
            for turn, plan in enumerate(outer)
        ]
        is_outer = ((layer == 0) & (group >= 2)) | ((layer == 3) & (group < 2))
        odd = group % 2 == 1
        inner_t = jnp.concatenate(
            [
                jnp.where(is_outer, jnp.where(odd, turned[p ^ 1], turned[p]), inner_t[p])
                for p in range(4)
            ],
            1,
        )
    else:
        inner_t = jnp.broadcast_to(mine_t, (layers, share, group_tokens))
        for turn, plan in enumerate(flat):
            inner_t = put(inner_t, follow(mine_t, plan), layer ^ turn)
        inner_t = inner_t.transpose(1, 0, 2).reshape(share, token_count)

    moved = []
    for step in range(lanes):
        part = lax.dynamic_slice_in_dim(grads_t, (lane + step) % lanes * share, share, 1)
        if step == 0:
            moved.append(send(part, lambda k, j, z: (z, j, k)))
        else:
            flip = layers // 2
            part = send(part, lambda k, j, z: (k ^ flip, (j + step) % lanes, z))
            moved.append(send(part, lambda k, j, z: (z, j, k ^ flip)))

    def layer_sum(value):
        for bit in bits:
            value = value + send(value, lambda k, j, z: (k, j, z ^ bit))
        return value

    def to_tokens(value):
        return merge(times(value, panel, 1, 1))

    def to_features(value):
        return merge(times(split(value * (1.0 / token_count), 0), panel, 1, 0))

    grads_split = split(grads_t, 0)
    u = to_tokens(grads_split)
    u = layer_sum(u)
    y = to_features(u) + damping * grads_t
    w = layer_sum(to_tokens(split(y, 0)))
    second = to_features(w) + damping * y
    solution_t = 3.0 * omega * grads_t - 3.0 * omega**2 * y + omega**3 * second

    u_near = jnp.where(group == layer, u, 0.0)
    for mask in range(1, layers):
        u_near = u_near + send(u, lambda k, j, z: (k ^ mask, j, z) if k == z else None)
    u_all = put(jnp.zeros((lanes,) + u.shape, u.dtype), u_near, lane)
    for step in range(1, lanes):
        u_all = put(u_all, shift(u_near, step), (lane - step) % lanes)
    u_all = u_all.reshape(lanes * u.shape[0], token_count)

    gram_tile = times(inner_t, panel, 1, 0) * (1.0 / token_count)

    grads_near = jnp.zeros((lanes,) + moved[0].shape, jnp.float32)
    for step in range(lanes):
        grads_near = put(grads_near, moved[step], (lane - step) % lanes)
    grads_near = grads_near.reshape(lanes * moved[0].shape[0], share)
    applied = times(inner_t, split(u_all * (1.0 / token_count), 0), 1, 1)
    columns = applied.shape[1] // 2
    applied = applied[:, :columns] + applied[:, columns:] + damping * grads_near.T
    return (gram_tile, applied, solution_t.T)


def solution(mesh):
    in_specs = (P("row", "col"), P("col", "row"))
    out_specs = (P("row", "col"), P("row", "col"), P("col", "row"))
    return jax.shard_map(step, mesh=mesh, in_specs=in_specs, out_specs=out_specs, check_vma=False)
```

time: 584 us -> 220 us (0.38)
  the two profiles are of different devices: /device:TPU:0 before, /device:TPU:4 now
where the time goes in v1:
time: 220 us; the launch traced here: 219 us
  waiting for transfers between devices  106 us (48%)
  starting transfers between devices  54.9 us (25%)
  matrix products  32.6 us (15%)
  local copies, waits for them, and re-layouts  17.3 us (8%)
  other arithmetic  7.16 us (3%)
    ppermute x28, waiting for transfers between devices, send(): return lax.ppermute(value, ('row', 'col'), pairs)  106 us
    ppermute x28, starting transfers between devices, send(): return lax.ppermute(value, ('row', 'col'), pairs)  54.9 us
    dot_general x6, matrix products, times(): lax.dot_general(left, right, (((left_dim,), (right_dim,)), ((), ())), pre...  32.6 us
    dynamic_update_slice x20, local copies, waits for them, and re-layouts, put(): lax.dynamic_update_slice(whole, part[(None,) * (whole.ndim - part.ndim)],...  8.23 us
  transfers between devices with their start and end apart: 28, of which 8 were waited for; matrix products, arithmetic and copies ran while one was open for 13% of the time, Pallas kernels for 0%

profile of v1, /device:TPU:4, one launch (start us, length us, event | category | flops | bytes accessed | tf_op | source)
XLA Modules:
  0.0 219.5 jit_solution(18311970913939650902)
XLA Ops:
  0.6 1.6 collective-permute-start.11
  2.3 1.9 collective-permute-start.13
  4.2 2.1 dynamic-slice_bitcast_fusion
  6.3 2.4 %reduce-precision_convert_fusion.1 = (bf16[64,4096]{1,0:T(8,128)(2,1)}, bf16[64,4096]{1,0:T(8,128)(2,1)}) fusion(f32[4096,64]{0,1:T(8,128)} %param.3), kind=kLoop, calls=%fused_computation.5 | loop fusion | flops 1048576 | bytes 2097152 | tf_op jit(solution)/shard_map/convert_element_type | solution.py:19
  8.6 2.5 %broadcast_in_dim.97 = bf16[4,2,64,4096]{3,2,1,0:T(8,128)(2,1)} broadcast(bf16[64,4096]{1,0:T(8,128)(2,1)S(1)} %copy-done.1), dimensions={2,3} | broadcast | bytes 4718592 | tf_op jit(solution)/shard_map/broadcast_in_dim | solution.py:109
  11.1 0.8 bitcast_dynamic-update-slice_fusion.9
  12.0 3.8 %collective-permute-done.11 = bf16[64,4096]{1,0:T(8,128)(2,1)} collective-permute-done((bf16[64,4096]{1,0:T(8,128)(2,1)}, bf16[64,4096]{1,0:T(8,128)(2,1)}, u32[]{:S(2)}, u32[]{:S(2)}) %collective-permute-start.11) | collective-permute-done | bytes 524320 | tf_op jit(solution)/shard_map/ppermute | solution.py:89
  15.8 4.4 %collective-permute-start.23 = (f32[64,2048]{1,0:T(8,128)S(1)}, f32[64,2048]{1,0:T(8,128)S(1)}, u32[]{:S(2)}, u32[]{:S(2)}) collective-permute-start(f32[64,2048]{1,0:T(8,128)S(1)} %get-tuple-element.24), channel_id=1, source_target_pairs={{0,0},{1,8},{2,16},{3,24},{4,4},{5,12},{6,20},{7,28},{8,1},{9,9},{... | collective-permute-start | bytes 1572872 | tf_op jit(solution)/shard_map/ppermute | solution.py:89
  20.3 0.9 bitcast_dynamic-update-slice_fusion.8
  21.2 1.9 bitcast_dynamic-update-slice_fusion.7
  23.2 20.3 %collective-permute-done.23 = f32[64,2048]{1,0:T(8,128)S(1)} collective-permute-done((f32[64,2048]{1,0:T(8,128)S(1)}, f32[64,2048]{1,0:T(8,128)S(1)}, u32[]{:S(2)}, u32[]{:S(2)}) %collective-permute-start.23) | collective-permute-done | bytes 524320 | tf_op jit(solution)/shard_map/ppermute | solution.py:89
  43.5 0.7 collective-permute-start.3
  44.3 0.7 collective-permute-start.2
  45.1 0.8 bitcast_dynamic-update-slice_fusion.6
  46.0 0.8 bitcast_dynamic-update-slice_fusion.5
  46.8 16.3 %collective-permute-start.1 = (bf16[2048,128]{0,1:T(8,128)(2,1)S(1)}, bf16[2048,128]{0,1:T(8,128)(2,1)S(1)}, u32[]{:S(2)}, u32[]{:S(2)}) collective-permute-start(bf16[2048,128]{0,1:T(8,128)(2,1)S(1)} %bitcast.107), channel_id=1, source_target_pairs={{0,2},{3,1},{4,6},{7,5},{8,10},{11,9},{12,14},{15,13},{16,18},{19,... | collective-permute-start | bytes 1572872 | tf_op jit(solution)/shard_map/ppermute | solution.py:89
  63.5 0.9 bitcast_dynamic-update-slice_fusion.4
  64.3 0.8 bitcast_dynamic-update-slice_fusion.3
  65.2 0.8 bitcast_dynamic-update-slice_fusion.2
  66.0 3.8 %fusion.8 = f32[128,512]{1,0:T(8,128)S(1)} fusion(bf16[512,4096]{1,0:T(8,128)(2,1)} %bitcast.32, bf16[64,4096]{1,0:T(8,128)(2,1)S(1)} %copy-done.5, bf16[64,4096]{1,0:T(8,128)(2,1)S(1)} %copy-done.4), kind=kOutput, calls=%fused_computation.17 | convolution fusion | flops 538968064 | bytes 5505024 | tf_op jit(solution)/shard_map/dot_general | solution.py:28
  69.8 2.8 %collective-permute-start.17 = (f32[64,512]{1,0:T(8,128)S(1)}, f32[64,512]{1,0:T(8,128)S(1)}, u32[]{:S(2)}, u32[]{:S(2)}) collective-permute-start(f32[64,512]{1,0:T(8,128)S(1)} %slice_add_fusion.4), channel_id=1, source_target_pairs={{0,1},{1,0},{2,3},{3,2},{4,5},{5,4},{6,7},{7,6},{8,9},{9,8},{10,11... | collective-permute-start | bytes 393224 | tf_op jit(solution)/shard_map/ppermute | solution.py:89
  72.7 31.0 %collective-permute-done.25 = f32[64,2048]{1,0:T(8,128)S(1)} collective-permute-done((f32[64,2048]{1,0:T(8,128)}, f32[64,2048]{1,0:T(8,128)S(1)}, u32[]{:S(2)}, u32[]{:S(2)}) %collective-permute-start.25) | collective-permute-done | bytes 524320 | tf_op jit(solution)/shard_map/ppermute | solution.py:89
  104.4 5.8 %collective-permute-done.18 = f32[64,512]{1,0:T(8,128)S(1)} collective-permute-done((f32[64,512]{1,0:T(8,128)S(1)}, f32[64,512]{1,0:T(8,128)S(1)}, u32[]{:S(2)}, u32[]{:S(2)}) %collective-permute-start.18) | collective-permute-done | bytes 131104 | tf_op jit(solution)/shard_map/ppermute | solution.py:89
  110.2 2.9 %fusion.28 = f32[128,4096]{1,0:T(8,128)S(1)} fusion(bf16[512,4096]{1,0:T(8,128)(2,1)} %bitcast.32, bf16[64,512]{1,0:T(8,128)(2,1)S(1)} %fusion.26, bf16[64,512]{1,0:T(8,128)(2,1)S(1)} %get-tuple-element.5), kind=kOutput, calls=%fused_computation.78 | convolution fusion | flops 537133056 | bytes 6422528 | tf_op jit(solution)/shard_map/dot_general | solution.py:28
  113.5 3.8 %fusion.12 = f32[128,512]{1,0:T(8,128)S(1)} fusion(bf16[512,4096]{1,0:T(8,128)(2,1)} %bitcast.32, bf16[64,4096]{1,0:T(8,128)(2,1)S(1)} %fusion.1, bf16[64,4096]{1,0:T(8,128)(2,1)S(1)} %get-tuple-element.3), kind=kOutput, calls=%fused_computation.21 | convolution fusion | flops 538968064 | bytes 5505024 | tf_op jit(solution)/shard_map/dot_general | solution.py:28
  117.3 0.7 slice_add_fusion.3
  117.9 2.0 collective-permute-start.26
  119.9 2.1 dynamic-slice_bitcast_fusion.9
  122.0 1.3 copy.7
  123.3 1.3 collective-permute-start.4
  124.6 1.3 collective-permute-start.10
  126.5 1.3 collective-permute-start.20
  127.9 0.7 collective-permute-start.19
  128.5 0.9 fusion.48
  129.5 1.3 collective-permute-start.9
  130.8 9.2 %collective-permute-done.20 = f32[64,512]{1,0:T(8,128)S(1)} collective-permute-done((f32[64,512]{1,0:T(8,128)S(1)}, f32[64,512]{1,0:T(8,128)S(1)}, u32[]{:S(2)}, u32[]{:S(2)}) %collective-permute-start.20) | collective-permute-done | bytes 131104 | tf_op jit(solution)/shard_map/ppermute | solution.py:89
  140.0 1.5 collective-permute-start.7
  141.7 9.0 %collective-permute-done.27 = f32[64,512]{1,0:T(8,128)S(1)} collective-permute-done((f32[64,512]{1,0:T(8,128)S(1)}, f32[64,512]{1,0:T(8,128)S(1)}, u32[]{:S(2)}, u32[]{:S(2)}) %collective-permute-start.27) | collective-permute-done | bytes 131104 | tf_op jit(solution)/shard_map/ppermute | solution.py:89
  150.7 2.9 %fusion.32 = f32[128,4096]{1,0:T(8,128)S(1)} fusion(bf16[512,4096]{1,0:T(8,128)(2,1)} %bitcast.32, bf16[64,512]{1,0:T(8,128)(2,1)S(1)} %get-tuple-element.28, bf16[64,512]{1,0:T(8,128)(2,1)S(1)} %get-tuple-element.27), kind=kOutput, calls=%fused_computation.82 | convolution fusion | flops 537133056 | bytes 6422528 | tf_op jit(solution)/shard_map/dot_general | solution.py:28
  153.6 1.3 fusion.5
  154.9 0.7 collective-permute-start.6
  155.7 13.7 %collective-permute-start.8 = (bf16[2048,128]{0,1:T(8,128)(2,1)S(1)}, bf16[2048,128]{0,1:T(8,128)(2,1)S(1)}, u32[]{:S(2)}, u32[]{:S(2)}) collective-permute-start(bf16[2048,128]{0,1:T(8,128)(2,1)S(1)} %copy-done.7), channel_id=1, source_target_pairs={{1,25},{2,26},{3,27},{5,29},{6,30},{7,31},{9,17},{10,18},{11,19},{... | collective-permute-start | bytes 1572872 | tf_op jit(solution)/shard_map/ppermute | solution.py:89
  169.7 1.5 collective-permute-start.5
  171.3 9.2 %collective-permute-done.8 = bf16[2048,128]{0,1:T(8,128)(2,1)S(1)} collective-permute-done((bf16[2048,128]{0,1:T(8,128)(2,1)S(1)}, bf16[2048,128]{0,1:T(8,128)(2,1)S(1)}, u32[]{:S(2)}, u32[]{:S(2)}) %collective-permute-start.8) | collective-permute-done | bytes 524320 | tf_op jit(solution)/shard_map/ppermute | solution.py:89
  180.6 17.8 %collective-permute-done.5 = bf16[2048,128]{0,1:T(8,128)(2,1)S(1)} collective-permute-done((bf16[2048,128]{0,1:T(8,128)(2,1)S(1)}, bf16[2048,128]{0,1:T(8,128)(2,1)S(1)}, u32[]{:S(2)}, u32[]{:S(2)}) %collective-permute-start.5) | collective-permute-done | bytes 524320 | tf_op jit(solution)/shard_map/ppermute | solution.py:89
  198.7 18.5 %convolution_multiply_fusion = f32[2048,4096]{1,0:T(8,128)} fusion(bf16[512,4096]{1,0:T(8,128)(2,1)} %bitcast.32, bf16[2048,128]{0,1:T(8,128)(2,1)S(1)} %get-tuple-element.13, bf16[2048,128]{0,1:T(8,128)(2,1)S(1)} %get-tuple-element.14, bf16[2048,128]{0,1:T(8,128)(2,1)S(1)} %get-tuple-element.10, bf16[2048,128]{0,1:T(8,128)(2,1)S(1)} %get-tuple-element.9), kind=kOutput, calls=%fused_computation | convolution fusion | flops 8606711808 | bytes 39845888 | tf_op jit(solution)/shard_map/dot_general | solution.py:28
  217.2 0.8 fusion.21
  218.4 1.1 fusion.7
  (78 shorter events, 3.9 us)
Async XLA Ops:
  0.6 8.0 %copy-start.1 = (bf16[64,4096]{1,0:T(8,128)(2,1)S(1)}, bf16[64,4096]{1,0:T(8,128)(2,1)}, u32[]{:S(2)}) copy-start(bf16[64,4096]{1,0:T(8,128)(2,1)} %param.2) | copy-start | bytes 1572868
  0.6 15.2 %collective-permute-start.11 = (bf16[64,4096]{1,0:T(8,128)(2,1)}, bf16[64,4096]{1,0:T(8,128)(2,1)}, u32[]{:S(2)}, u32[]{:S(2)}) collective-permute-start(bf16[64,4096]{1,0:T(8,128)(2,1)} %param.2), channel_id=1, source_target_pairs={{0,8},{1,9},{2,10},{3,11},{4,12},{5,13},{6,14},{7,15},{8,0},{9,1},... | collective-permute-start | bytes 1572872 | tf_op jit(solution)/shard_map/ppermute | solution.py:89
  2.2 18.1 %collective-permute-start = (bf16[64,4096]{1,0:T(8,128)(2,1)}, bf16[64,4096]{1,0:T(8,128)(2,1)S(1)}, u32[]{:S(2)}, u32[]{:S(2)}) collective-permute-start(bf16[64,4096]{1,0:T(8,128)(2,1)} %param.2), channel_id=1, source_target_pairs={{0,4},{1,5},{2,6},{3,7},{4,0},{5,1},{6,2},{7,3},{8,12},{9,13},{10,... | collective-permute-start | bytes 1572872 | tf_op jit(solution)/shard_map/ppermute | solution.py:89
  2.2 44.6 %collective-permute-start.15 = (bf16[64,4096]{1,0:T(8,128)(2,1)}, bf16[64,4096]{1,0:T(8,128)(2,1)S(1)}, u32[]{:S(2)}, u32[]{:S(2)}) collective-permute-start(bf16[64,4096]{1,0:T(8,128)(2,1)} %param.2), channel_id=1, source_target_pairs={{0,24},{1,25},{2,26},{3,27},{4,28},{5,29},{6,30},{7,31},{8,16},{9,... | collective-permute-start | bytes 1572872 | tf_op jit(solution)/shard_map/ppermute | solution.py:89
  2.3 42.0 %collective-permute-start.13 = (bf16[64,4096]{1,0:T(8,128)(2,1)}, bf16[64,4096]{1,0:T(8,128)(2,1)S(1)}, u32[]{:S(2)}, u32[]{:S(2)}) collective-permute-start(bf16[64,4096]{1,0:T(8,128)(2,1)} %param.2), channel_id=1, source_target_pairs={{0,16},{1,17},{2,18},{3,19},{4,20},{5,21},{6,22},{7,23},{8,24},{9,... | collective-permute-start | bytes 1572872 | tf_op jit(solution)/shard_map/ppermute | solution.py:89
  6.3 56.9 %collective-permute-start.24 = (f32[64,2048]{1,0:T(8,128)}, f32[64,2048]{1,0:T(8,128)}, u32[]{:S(2)}, u32[]{:S(2)}) collective-permute-start(f32[64,2048]{1,0:T(8,128)} %get-tuple-element.23), channel_id=1, source_target_pairs={{0,20},{1,21},{2,22},{3,23},{4,16},{5,17},{6,18},{7,19},{8,28},{9,... | collective-permute-start | bytes 1572872 | tf_op jit(solution)/shard_map/ppermute | solution.py:89
  15.8 27.7 %collective-permute-start.23 = (f32[64,2048]{1,0:T(8,128)S(1)}, f32[64,2048]{1,0:T(8,128)S(1)}, u32[]{:S(2)}, u32[]{:S(2)}) collective-permute-start(f32[64,2048]{1,0:T(8,128)S(1)} %get-tuple-element.24), channel_id=1, source_target_pairs={{0,0},{1,8},{2,16},{3,24},{4,4},{5,12},{6,20},{7,28},{8,1},{9,9},{... | collective-permute-start | bytes 1572872 | tf_op jit(solution)/shard_map/ppermute | solution.py:89
  20.3 24.8 %collective-permute-start.12 = (bf16[64,4096]{1,0:T(8,128)(2,1)}, bf16[64,4096]{1,0:T(8,128)(2,1)S(1)}, u32[]{:S(2)}, u32[]{:S(2)}) collective-permute-start(bf16[64,4096]{1,0:T(8,128)(2,1)} %collective-permute-done.11), channel_id=1, source_target_pairs={{0,4},{1,5},{2,6},{3,7},{4,0},{5,1},{6,2},{7,3},{8,12},{9,13},{10,... | collective-permute-start | bytes 1572872 | tf_op jit(solution)/shard_map/ppermute | solution.py:89
  23.1 42.9 %copy-start.4 = (bf16[64,4096]{1,0:T(8,128)(2,1)S(1)}, bf16[64,4096]{1,0:T(8,128)(2,1)}, u32[]{:S(2)}) copy-start(bf16[64,4096]{1,0:T(8,128)(2,1)} %get-tuple-element.25) | copy-start | bytes 1572868
  23.1 42.9 %copy-start.5 = (bf16[64,4096]{1,0:T(8,128)(2,1)S(1)}, bf16[64,4096]{1,0:T(8,128)(2,1)}, u32[]{:S(2)}) copy-start(bf16[64,4096]{1,0:T(8,128)(2,1)} %get-tuple-element.26) | copy-start | bytes 1572868
  43.5 60.6 %collective-permute-start.3 = (bf16[2048,128]{0,1:T(8,128)(2,1)S(1)}, bf16[2048,128]{0,1:T(8,128)(2,1)S(1)}, u32[]{:S(2)}, u32[]{:S(2)}) collective-permute-start(bf16[2048,128]{0,1:T(8,128)(2,1)S(1)} %bitcast.105), channel_id=1, source_target_pairs={{0,1},{1,0},{2,3},{3,2},{4,5},{5,4},{6,7},{7,6},{8,9},{9,8},{10,11... | collective-permute-start | bytes 1572872 | tf_op jit(solution)/shard_map/ppermute | solution.py:89
  44.3 59.7 %collective-permute-start.2 = (bf16[2048,128]{0,1:T(8,128)(2,1)S(1)}, bf16[2048,128]{0,1:T(8,128)(2,1)S(1)}, u32[]{:S(2)}, u32[]{:S(2)}) collective-permute-start(bf16[2048,128]{0,1:T(8,128)(2,1)S(1)} %bitcast.106), channel_id=1, source_target_pairs={{1,2},{2,1},{5,6},{6,5},{9,10},{10,9},{13,14},{14,13},{17,18},{18,... | collective-permute-start | bytes 1572872 | tf_op jit(solution)/shard_map/ppermute | solution.py:89
  45.1 18.4 %collective-permute-start.14 = (bf16[64,4096]{1,0:T(8,128)(2,1)S(1)}, bf16[64,4096]{1,0:T(8,128)(2,1)S(1)}, u32[]{:S(2)}, u32[]{:S(2)}) collective-permute-start(bf16[64,4096]{1,0:T(8,128)(2,1)S(1)} %collective-permute-done.13), channel_id=1, source_target_pairs={{0,4},{1,5},{2,6},{3,7},{4,0},{5,1},{6,2},{7,3},{8,12},{9,13},{10,... | collective-permute-start | bytes 1572872 | tf_op jit(solution)/shard_map/ppermute | solution.py:89
  46.8 56.9 %collective-permute-start.1 = (bf16[2048,128]{0,1:T(8,128)(2,1)S(1)}, bf16[2048,128]{0,1:T(8,128)(2,1)S(1)}, u32[]{:S(2)}, u32[]{:S(2)}) collective-permute-start(bf16[2048,128]{0,1:T(8,128)(2,1)S(1)} %bitcast.107), channel_id=1, source_target_pairs={{0,2},{3,1},{4,6},{7,5},{8,10},{11,9},{12,14},{15,13},{16,18},{19,... | collective-permute-start | bytes 1572872 | tf_op jit(solution)/shard_map/ppermute | solution.py:89
  63.1 2.0 collective-permute-start.16
  63.5 40.2 %collective-permute-start.25 = (f32[64,2048]{1,0:T(8,128)}, f32[64,2048]{1,0:T(8,128)S(1)}, u32[]{:S(2)}, u32[]{:S(2)}) collective-permute-start(f32[64,2048]{1,0:T(8,128)} %collective-permute-done.24), channel_id=1, source_target_pairs={{0,2},{1,10},{2,18},{3,26},{4,6},{5,14},{6,22},{7,30},{8,3},{9,11}... | collective-permute-start | bytes 1572872 | tf_op jit(solution)/shard_map/ppermute | solution.py:89
  69.8 34.4 %collective-permute-start.17 = (f32[64,512]{1,0:T(8,128)S(1)}, f32[64,512]{1,0:T(8,128)S(1)}, u32[]{:S(2)}, u32[]{:S(2)}) collective-permute-start(f32[64,512]{1,0:T(8,128)S(1)} %slice_add_fusion.4), channel_id=1, source_target_pairs={{0,1},{1,0},{2,3},{3,2},{4,5},{5,4},{6,7},{7,6},{8,9},{9,8},{10,11... | collective-permute-start | bytes 393224 | tf_op jit(solution)/shard_map/ppermute | solution.py:89
  104.2 8.9 %copy-start = (f32[4096,64]{0,1:T(8,128)S(1)}, f32[4096,64]{0,1:T(8,128)}, u32[]{:S(2)}) copy-start(f32[4096,64]{0,1:T(8,128)} %param.3) | copy-start | bytes 3145732
  104.2 5.9 %collective-permute-start.18 = (f32[64,512]{1,0:T(8,128)S(1)}, f32[64,512]{1,0:T(8,128)S(1)}, u32[]{:S(2)}, u32[]{:S(2)}) collective-permute-start(f32[64,512]{1,0:T(8,128)S(1)} %fusion.49), channel_id=1, source_target_pairs={{0,2},{1,3},{2,0},{3,1},{4,6},{5,7},{6,4},{7,5},{8,10},{9,11},{10,... | collective-permute-start | bytes 393224 | tf_op jit(solution)/shard_map/ppermute | solution.py:89
  117.9 9.9 %collective-permute-start.26 = (f32[64,512]{1,0:T(8,128)}, f32[64,512]{1,0:T(8,128)}, u32[]{:S(2)}, u32[]{:S(2)}) collective-permute-start(f32[64,512]{1,0:T(8,128)} %slice_add_fusion.3), channel_id=1, source_target_pairs={{0,1},{1,0},{2,3},{3,2},{4,5},{5,4},{6,7},{7,6},{8,9},{9,8},{10,11... | collective-permute-start | bytes 393224 | tf_op jit(solution)/shard_map/ppermute | solution.py:89
  123.3 57.3 %collective-permute-start.4 = (bf16[2048,128]{0,1:T(8,128)(2,1)}, bf16[2048,128]{0,1:T(8,128)(2,1)S(1)}, u32[]{:S(2)}, u32[]{:S(2)}) collective-permute-start(bf16[2048,128]{0,1:T(8,128)(2,1)} %get-tuple-element.15), channel_id=1, source_target_pairs={{1,24},{2,11},{5,28},{6,15},{9,16},{10,3},{13,20},{14,7}} | collective-permute-start | bytes 1572872 | tf_op jit(solution)/shard_map/ppermute | solution.py:89
  124.6 56.0 %collective-permute-start.10 = (bf16[2048,128]{0,1:T(8,128)(2,1)}, bf16[2048,128]{0,1:T(8,128)(2,1)S(1)}, u32[]{:S(2)}, u32[]{:S(2)}) collective-permute-start(bf16[2048,128]{0,1:T(8,128)(2,1)} %get-tuple-element.16), channel_id=1, source_target_pairs={{17,16},{18,3},{21,20},{22,7},{25,24},{26,11},{29,28},{30,15}} | collective-permute-start | bytes 1572872 | tf_op jit(solution)/shard_map/ppermute | solution.py:89
  125.9 3.6 %collective-permute-start.21 = (f32[64,512]{1,0:T(8,128)S(1)}, f32[64,512]{1,0:T(8,128)S(1)}, u32[]{:S(2)}, u32[]{:S(2)}) collective-permute-start(f32[64,512]{1,0:T(8,128)S(1)} %get-tuple-element.6), channel_id=1, source_target_pairs={{0,24},{4,28},{9,17},{13,21},{18,10},{22,14},{27,3},{31,7}} | collective-permute-start | bytes 393224 | tf_op jit(solution)/shard_map/ppermute | solution.py:89
  126.5 13.5 %collective-permute-start.20 = (f32[64,512]{1,0:T(8,128)S(1)}, f32[64,512]{1,0:T(8,128)S(1)}, u32[]{:S(2)}, u32[]{:S(2)}) collective-permute-start(f32[64,512]{1,0:T(8,128)S(1)} %get-tuple-element.6), channel_id=1, source_target_pairs={{0,16},{4,20},{9,25},{13,29},{18,2},{22,6},{27,11},{31,15}} | collective-permute-start | bytes 393224 | tf_op jit(solution)/shard_map/ppermute | solution.py:89
  127.9 13.7 %collective-permute-start.19 = (f32[64,512]{1,0:T(8,128)S(1)}, f32[64,512]{1,0:T(8,128)S(1)}, u32[]{:S(2)}, u32[]{:S(2)}) collective-permute-start(f32[64,512]{1,0:T(8,128)S(1)} %get-tuple-element.6), channel_id=1, source_target_pairs={{0,8},{4,12},{9,1},{13,5},{18,26},{22,30},{27,19},{31,23}} | collective-permute-start | bytes 393224 | tf_op jit(solution)/shard_map/ppermute | solution.py:89
  129.5 51.1 %collective-permute-start.9 = (bf16[2048,128]{0,1:T(8,128)(2,1)}, bf16[2048,128]{0,1:T(8,128)(2,1)S(1)}, u32[]{:S(2)}, u32[]{:S(2)}) collective-permute-start(bf16[2048,128]{0,1:T(8,128)(2,1)} %get-tuple-element.17), channel_id=1, source_target_pairs={{17,24},{18,11},{21,28},{22,15},{25,16},{26,3},{29,20},{30,7}} | collective-permute-start | bytes 1572872 | tf_op jit(solution)/shard_map/ppermute | solution.py:89
  140.0 29.7 %collective-permute-start.7 = (bf16[2048,128]{0,1:T(8,128)(2,1)}, bf16[2048,128]{0,1:T(8,128)(2,1)S(1)}, u32[]{:S(2)}, u32[]{:S(2)}) collective-permute-start(bf16[2048,128]{0,1:T(8,128)(2,1)} %get-tuple-element.19), channel_id=1, source_target_pairs={{1,17},{2,18},{3,19},{5,21},{6,22},{7,23},{9,25},{10,26},{11,27},{... | collective-permute-start | bytes 1572872 | tf_op jit(solution)/shard_map/ppermute | solution.py:89
  141.5 9.1 %collective-permute-start.27 = (f32[64,512]{1,0:T(8,128)S(1)}, f32[64,512]{1,0:T(8,128)S(1)}, u32[]{:S(2)}, u32[]{:S(2)}) collective-permute-start(f32[64,512]{1,0:T(8,128)S(1)} %fusion.48), channel_id=1, source_target_pairs={{0,2},{1,3},{2,0},{3,1},{4,6},{5,7},{6,4},{7,5},{8,10},{9,11},{10,... | collective-permute-start | bytes 393224 | tf_op jit(solution)/shard_map/ppermute | solution.py:89
  150.7 4.3 %collective-permute-start.22 = (f32[64,512]{1,0:T(8,128)S(1)}, f32[64,512]{1,0:T(8,128)S(1)}, u32[]{:S(2)}, u32[]{:S(2)}) collective-permute-start(f32[64,512]{1,0:T(8,128)S(1)} %get-tuple-element.8), channel_id=1, source_target_pairs={{0,4},{1,5},{2,6},{3,7},{4,0},{5,1},{6,2},{7,3},{8,12},{9,13},{10,... | collective-permute-start | bytes 393224 | tf_op jit(solution)/shard_map/ppermute | solution.py:89
  153.6 1.3 copy-start.8
  153.6 2.1 copy-start.7
  153.6 15.8 %copy-start.3 = (bf16[2048,128]{0,1:T(8,128)(2,1)S(1)}, bf16[2048,128]{0,1:T(8,128)(2,1)}, u32[]{:S(2)}) copy-start(bf16[2048,128]{0,1:T(8,128)(2,1)} %get-tuple-element.21) | copy-start | bytes 1572868
  153.6 16.1 %copy-start.6 = (bf16[2048,128]{0,1:T(8,128)(2,1)S(1)}, bf16[2048,128]{0,1:T(8,128)(2,1)}, u32[]{:S(2)}) copy-start(bf16[2048,128]{0,1:T(8,128)(2,1)} %get-tuple-element.22) | copy-start | bytes 1572868
  154.9 0.8 collective-permute-start.6
  155.7 24.8 %collective-permute-start.8 = (bf16[2048,128]{0,1:T(8,128)(2,1)S(1)}, bf16[2048,128]{0,1:T(8,128)(2,1)S(1)}, u32[]{:S(2)}, u32[]{:S(2)}) collective-permute-start(bf16[2048,128]{0,1:T(8,128)(2,1)S(1)} %copy-done.7), channel_id=1, source_target_pairs={{1,25},{2,26},{3,27},{5,29},{6,30},{7,31},{9,17},{10,18},{11,19},{... | collective-permute-start | bytes 1572872 | tf_op jit(solution)/shard_map/ppermute | solution.py:89
  169.7 28.7 %collective-permute-start.5 = (bf16[2048,128]{0,1:T(8,128)(2,1)S(1)}, bf16[2048,128]{0,1:T(8,128)(2,1)S(1)}, u32[]{:S(2)}, u32[]{:S(2)}) collective-permute-start(bf16[2048,128]{0,1:T(8,128)(2,1)S(1)} %copy-done.6), channel_id=1, source_target_pairs={{1,16},{2,3},{5,20},{6,7},{9,24},{10,11},{13,28},{14,15}} | collective-permute-start | bytes 1572872 | tf_op jit(solution)/shard_map/ppermute | solution.py:89
  217.2 1.2 copy-start.2

commit v2 on v1

--- a/solution.py
+++ b/solution.py
@@ -168,15 +168,14 @@
             inner_t = put(inner_t, follow(mine_t, plan), layer ^ turn)
         inner_t = inner_t.transpose(1, 0, 2).reshape(share, token_count)
 
-    moved = []
-    for step in range(lanes):
-        part = lax.dynamic_slice_in_dim(grads_t, (lane + step) % lanes * share, share, 1)
-        if step == 0:
-            moved.append(send(part, lambda k, j, z: (z, j, k)))
-        else:
-            flip = layers // 2
-            part = send(part, lambda k, j, z: (k ^ flip, (j + step) % lanes, z))
-            moved.append(send(part, lambda k, j, z: (z, j, k ^ flip)))
+    def by_lane(parts):
+        rows = []
+        for j in range(lanes):
+            row = parts[0]
+            for step in range(1, lanes):
+                row = jnp.where((lane - step) % lanes == j, parts[step], row)
+            rows.append(row)
+        return jnp.concatenate(rows, 0)
 
     def layer_sum(value):
         for bit in bits:
@@ -197,23 +196,19 @@
     second = to_features(w) + damping * y
     solution_t = 3.0 * omega * grads_t - 3.0 * omega**2 * y + omega**3 * second
 
-    u_near = jnp.where(group == layer, u, 0.0)
-    for mask in range(1, layers):
-        u_near = u_near + send(u, lambda k, j, z: (k ^ mask, j, z) if k == z else None)
-    u_all = put(jnp.zeros((lanes,) + u.shape, u.dtype), u_near, lane)
-    for step in range(1, lanes):
-        u_all = put(u_all, shift(u_near, step), (lane - step) % lanes)
-    u_all = u_all.reshape(lanes * u.shape[0], token_count)
+    moved = []
+    for step in range(lanes):
+        part = lax.dynamic_slice_in_dim(y, (lane + step) % lanes * share, share, 1)
+        if step == 0:
+            moved.append(send(part, lambda k, j, z: (z, j, k)))
+        else:
+            flips = [layers // 2 >> j % 2 for j in range(lanes)]
+            part = send(part, lambda k, j, z: (k ^ flips[j], (j + step) % lanes, z))
+            moved.append(send(part, lambda k, j, z: (z, j, k ^ flips[(j - step) % lanes])))
+    applied = by_lane(moved).T
 
     gram_tile = times(inner_t, panel, 1, 0) * (1.0 / token_count)
 
-    grads_near = jnp.zeros((lanes,) + moved[0].shape, jnp.float32)
-    for step in range(lanes):
-        grads_near = put(grads_near, moved[step], (lane - step) % lanes)
-    grads_near = grads_near.reshape(lanes * moved[0].shape[0], share)
-    applied = times(inner_t, split(u_all * (1.0 / token_count), 0), 1, 1)
-    columns = applied.shape[1] // 2
-    applied = applied[:, :columns] + applied[:, columns:] + damping * grads_near.T
     return (gram_tile, applied, solution_t.T)
 
 

time: 220 us -> 159 us (0.72)
  the two profiles are of different devices: /device:TPU:4 before, /device:TPU:0 now
where the time goes in v2:
time: 159 us; the launch traced here: 157 us
  waiting for transfers between devices  59.1 us (37%)
  starting transfers between devices  47 us (30%)
  matrix products  31.7 us (20%)
  local copies, waits for them, and re-layouts  13.1 us (8%)
  other arithmetic  4.33 us (3%)
    ppermute x24, waiting for transfers between devices, send(): return lax.ppermute(value, ('row', 'col'), pairs)  59.1 us
    ppermute x24, starting transfers between devices, send(): return lax.ppermute(value, ('row', 'col'), pairs)  47 us
    dot_general x5, matrix products, times(): lax.dot_general(left, right, (((left_dim,), (right_dim,)), ((), ())), pre...  31.7 us
    dynamic_update_slice x17, local copies, waits for them, and re-layouts, put(): lax.dynamic_update_slice(whole, part[(None,) * (whole.ndim - part.ndim)],...  7.03 us
    broadcast_in_dim x1, local copies, waits for them, and re-layouts, step(): panel = jnp.broadcast_to(acts, (layers, lanes, tokens, width))  3.53 us
  transfers between devices with their start and end apart: 24, of which 11 were waited for; matrix products, arithmetic and copies ran while one was open for 26% of the time, Pallas kernels for 0%

profile of v2, /device:TPU:0, one launch (start us, length us, event | category | flops | bytes accessed | tf_op | source)
XLA Modules:
  0.0 156.5 jit_solution(2303513875065185733)
XLA Ops:
  0.6 3.0 %collective-permute-start.11 = (bf16[64,4096]{1,0:T(8,128)(2,1)}, bf16[64,4096]{1,0:T(8,128)(2,1)S(1)}, u32[]{:S(2)}, u32[]{:S(2)}) collective-permute-start(bf16[64,4096]{1,0:T(8,128)(2,1)} %param.2), channel_id=1, source_target_pairs={{0,8},{1,9},{2,10},{3,11},{4,12},{5,13},{6,14},{7,15},{8,0},{9,1},... | collective-permute-start | bytes 1572872 | tf_op jit(solution)/shard_map/ppermute | solution.py:89
  3.7 1.5 collective-permute-start.15
  5.3 2.2 %reduce-precision_convert_fusion.1 = (bf16[64,4096]{1,0:T(8,128)(2,1)S(1)}, bf16[64,4096]{1,0:T(8,128)(2,1)}) fusion(f32[4096,64]{0,1:T(8,128)} %param.3), kind=kLoop, calls=%fused_computation.11 | loop fusion | flops 1048576 | bytes 2097152 | tf_op jit(solution)/shard_map/convert_element_type | solution.py:19
  7.5 3.5 %broadcast_in_dim.75 = bf16[4,2,64,4096]{3,2,1,0:T(8,128)(2,1)} broadcast(bf16[64,4096]{1,0:T(8,128)(2,1)} %param.2), dimensions={2,3} | broadcast | bytes 4718592 | tf_op jit(solution)/shard_map/broadcast_in_dim | solution.py:109
  11.0 0.8 bitcast_dynamic-update-slice_fusion.7
  12.1 2.0 %collective-permute-start.3 = (bf16[2048,128]{0,1:T(8,128)(2,1)S(1)}, bf16[2048,128]{0,1:T(8,128)(2,1)S(1)}, u32[]{:S(2)}, u32[]{:S(2)}) collective-permute-start(bf16[2048,128]{0,1:T(8,128)(2,1)S(1)} %bitcast.89), channel_id=1, source_target_pairs={{0,1},{1,0},{2,3},{3,2},{4,5},{5,4},{6,7},{7,6},{8,9},{9,8},{10,11... | collective-permute-start | bytes 1572872 | tf_op jit(solution)/shard_map/ppermute | solution.py:89
  14.2 0.7 collective-permute-start.2
  14.9 1.8 %collective-permute-done.11 = bf16[64,4096]{1,0:T(8,128)(2,1)S(1)} collective-permute-done((bf16[64,4096]{1,0:T(8,128)(2,1)}, bf16[64,4096]{1,0:T(8,128)(2,1)S(1)}, u32[]{:S(2)}, u32[]{:S(2)}) %collective-permute-start.11) | collective-permute-done | bytes 524320 | tf_op jit(solution)/shard_map/ppermute | solution.py:89
  16.7 0.8 bitcast_dynamic-update-slice_fusion.6
  17.5 0.8 bitcast_dynamic-update-slice_fusion.5
  18.3 10.0 %collective-permute-done.15 = bf16[64,4096]{1,0:T(8,128)(2,1)S(1)} collective-permute-done((bf16[64,4096]{1,0:T(8,128)(2,1)}, bf16[64,4096]{1,0:T(8,128)(2,1)S(1)}, u32[]{:S(2)}, u32[]{:S(2)}) %collective-permute-start.15) | collective-permute-done | bytes 524320 | tf_op jit(solution)/shard_map/ppermute | solution.py:89
  28.4 4.5 %collective-permute-start.1 = (bf16[2048,128]{0,1:T(8,128)(2,1)S(1)}, bf16[2048,128]{0,1:T(8,128)(2,1)S(1)}, u32[]{:S(2)}, u32[]{:S(2)}) collective-permute-start(bf16[2048,128]{0,1:T(8,128)(2,1)S(1)} %bitcast.91), channel_id=1, source_target_pairs={{0,2},{3,1},{4,6},{7,5},{8,10},{11,9},{12,14},{15,13},{16,18},{19,... | collective-permute-start | bytes 1572872 | tf_op jit(solution)/shard_map/ppermute | solution.py:89
  33.0 0.5 collective-permute-start.14
  33.5 0.8 bitcast_dynamic-update-slice_fusion.4
  34.3 0.8 bitcast_dynamic-update-slice_fusion.3
  35.1 0.5 collective-permute-done.14
  35.6 0.8 bitcast_dynamic-update-slice_fusion.2
  36.4 0.8 bitcast_dynamic-update-slice_fusion.1
  37.3 0.8 bitcast_dynamic-update-slice_fusion
  38.1 3.7 %fusion.14 = f32[128,512]{1,0:T(8,128)S(1)} fusion(bf16[512,4096]{1,0:T(8,128)(2,1)} %bitcast.32, bf16[64,4096]{1,0:T(8,128)(2,1)S(1)} %copy-done.2, bf16[64,4096]{1,0:T(8,128)(2,1)S(1)} %get-tuple-element.26), kind=kOutput, calls=%fused_computation.21 | convolution fusion | flops 538968064 | bytes 5505024 | tf_op jit(solution)/shard_map/dot_general | solution.py:28
  42.0 1.7 %collective-permute-done.1 = bf16[2048,128]{0,1:T(8,128)(2,1)S(1)} collective-permute-done((bf16[2048,128]{0,1:T(8,128)(2,1)S(1)}, bf16[2048,128]{0,1:T(8,128)(2,1)S(1)}, u32[]{:S(2)}, u32[]{:S(2)}) %collective-permute-start.1) | collective-permute-done | bytes 524320 | tf_op jit(solution)/shard_map/ppermute | solution.py:89
  43.7 0.2 broadcast_in_dim.66
  44.1 3.3 %collective-permute-done.17 = f32[64,512]{1,0:T(8,128)S(1)} collective-permute-done((f32[64,512]{1,0:T(8,128)S(1)}, f32[64,512]{1,0:T(8,128)S(1)}, u32[]{:S(2)}, u32[]{:S(2)}) %collective-permute-start.17) | collective-permute-done | bytes 131104 | tf_op jit(solution)/shard_map/ppermute | solution.py:89
  47.5 0.8 collective-permute-start.18
  48.4 7.6 %collective-permute-done.18 = f32[64,512]{1,0:T(8,128)S(1)} collective-permute-done((f32[64,512]{1,0:T(8,128)S(1)}, f32[64,512]{1,0:T(8,128)S(1)}, u32[]{:S(2)}, u32[]{:S(2)}) %collective-permute-start.18) | collective-permute-done | bytes 131104 | tf_op jit(solution)/shard_map/ppermute | solution.py:89
  56.0 2.9 %fusion.29 = f32[128,4096]{1,0:T(8,128)S(1)} fusion(bf16[512,4096]{1,0:T(8,128)(2,1)} %bitcast.32, bf16[64,512]{1,0:T(8,128)(2,1)S(1)} %get-tuple-element.31, bf16[64,512]{1,0:T(8,128)(2,1)S(1)} %get-tuple-element.30), kind=kOutput, calls=%fused_computation.74 | convolution fusion | flops 537133056 | bytes 6422528 | tf_op jit(solution)/shard_map/dot_general | solution.py:28
  59.3 3.7 %fusion.18 = f32[128,512]{1,0:T(8,128)S(1)} fusion(bf16[512,4096]{1,0:T(8,128)(2,1)} %bitcast.32, bf16[64,4096]{1,0:T(8,128)(2,1)S(1)} %fusion.8, bf16[64,4096]{1,0:T(8,128)(2,1)S(1)} %get-tuple-element.6), kind=kOutput, calls=%fused_computation.26 | convolution fusion | flops 538968064 | bytes 5505024 | tf_op jit(solution)/shard_map/dot_general | solution.py:28
  63.1 0.6 dynamic-slice_bitcast_fusion.7
  63.7 0.7 collective-permute-start.4
  64.4 0.7 collective-permute-start.10
  65.1 0.7 collective-permute-start.9
  65.8 1.3 collective-permute-start.7
  67.2 0.9 collective-permute-done.22
  68.1 6.5 %collective-permute-start.23 = (f32[64,512]{1,0:T(8,128)S(1)}, f32[64,512]{1,0:T(8,128)S(1)}, u32[]{:S(2)}, u32[]{:S(2)}) collective-permute-start(f32[64,512]{1,0:T(8,128)S(1)} %fusion.48), channel_id=1, source_target_pairs={{0,2},{1,3},{2,0},{3,1},{4,6},{5,7},{6,4},{7,5},{8,10},{9,11},{10,... | collective-permute-start | bytes 393224 | tf_op jit(solution)/shard_map/ppermute | solution.py:89
  74.7 5.3 %collective-permute-done.23 = f32[64,512]{1,0:T(8,128)S(1)} collective-permute-done((f32[64,512]{1,0:T(8,128)S(1)}, f32[64,512]{1,0:T(8,128)S(1)}, u32[]{:S(2)}, u32[]{:S(2)}) %collective-permute-start.23) | collective-permute-done | bytes 131104 | tf_op jit(solution)/shard_map/ppermute | solution.py:89
  80.0 2.5 %collective-permute-start.6 = (bf16[2048,128]{0,1:T(8,128)(2,1)S(1)}, bf16[2048,128]{0,1:T(8,128)(2,1)S(1)}, u32[]{:S(2)}, u32[]{:S(2)}) collective-permute-start(bf16[2048,128]{0,1:T(8,128)(2,1)S(1)} %get-tuple-element.19), channel_id=1, source_target_pairs={{0,8},{1,9},{2,10},{4,12},{5,13},{6,14},{8,0},{9,1},{10,2},{12,4},... | collective-permute-start | bytes 1572872 | tf_op jit(solution)/shard_map/ppermute | solution.py:89
  82.5 2.9 %fusion.33 = f32[128,4096]{1,0:T(8,128)S(1)} fusion(bf16[512,4096]{1,0:T(8,128)(2,1)} %bitcast.32, bf16[64,512]{1,0:T(8,128)(2,1)S(1)} %get-tuple-element.29, bf16[64,512]{1,0:T(8,128)(2,1)S(1)} %get-tuple-element.28), kind=kOutput, calls=%fused_computation.78 | convolution fusion | flops 537133056 | bytes 6422528 | tf_op jit(solution)/shard_map/dot_general | solution.py:28
  85.5 1.3 fusion.12
  86.7 7.6 %collective-permute-done.6 = bf16[2048,128]{0,1:T(8,128)(2,1)S(1)} collective-permute-done((bf16[2048,128]{0,1:T(8,128)(2,1)S(1)}, bf16[2048,128]{0,1:T(8,128)(2,1)S(1)}, u32[]{:S(2)}, u32[]{:S(2)}) %collective-permute-start.6) | collective-permute-done | bytes 524320 | tf_op jit(solution)/shard_map/ppermute | solution.py:89
  94.3 1.3 collective-permute-start.8
  95.6 0.2 broadcast_in_dim.71
  95.9 0.7 collective-permute-start.5
  96.7 12.0 %collective-permute-done.8 = bf16[2048,128]{0,1:T(8,128)(2,1)S(1)} collective-permute-done((bf16[2048,128]{0,1:T(8,128)(2,1)S(1)}, bf16[2048,128]{0,1:T(8,128)(2,1)S(1)}, u32[]{:S(2)}, u32[]{:S(2)}) %collective-permute-start.8) | collective-permute-done | bytes 524320 | tf_op jit(solution)/shard_map/ppermute | solution.py:89
  108.7 0.7 collective-permute-start.21
  109.7 8.3 %collective-permute-done.19 = f32[64,2048]{1,0:T(8,128)S(1)} collective-permute-done((f32[64,2048]{1,0:T(8,128)S(1)}, f32[64,2048]{1,0:T(8,128)S(1)}, u32[]{:S(2)}, u32[]{:S(2)}) %collective-permute-start.19) | collective-permute-done | bytes 524320 | tf_op jit(solution)/shard_map/ppermute | solution.py:89
  118.1 18.5 %collective-permute-start.20 = (f32[64,2048]{1,0:T(8,128)S(1)}, f32[64,2048]{1,0:T(8,128)S(1)}, u32[]{:S(2)}, u32[]{:S(2)}) collective-permute-start(f32[64,2048]{1,0:T(8,128)S(1)} %collective-permute-done.19), channel_id=1, source_target_pairs={{0,1},{1,9},{2,17},{3,25},{4,6},{5,14},{6,22},{7,30},{8,0},{9,8},{... | collective-permute-start | bytes 1572872 | tf_op jit(solution)/shard_map/ppermute | solution.py:89
  136.6 18.4 %convolution_multiply_fusion = f32[2048,4096]{1,0:T(8,128)} fusion(bf16[512,4096]{1,0:T(8,128)(2,1)} %bitcast.32, bf16[2048,128]{0,1:T(8,128)(2,1)S(1)} %get-tuple-element.12, bf16[2048,128]{0,1:T(8,128)(2,1)S(1)} %get-tuple-element.13, bf16[2048,128]{0,1:T(8,128)(2,1)S(1)} %get-tuple-element.9, bf16[2048,128]{0,1:T(8,128)(2,1)S(1)} %get-tuple-element.8), kind=kOutput, calls=%fused_computation | convolution fusion | flops 8606711808 | bytes 39845888 | tf_op jit(solution)/shard_map/dot_general | solution.py:28
  155.2 1.3 copy.5
  (49 shorter events, 1.9 us)
Async XLA Ops:
  0.6 10.4 %copy-start.1 = (bf16[64,4096]{1,0:T(8,128)(2,1)S(1)}, bf16[64,4096]{1,0:T(8,128)(2,1)}, u32[]{:S(2)}) copy-start(bf16[64,4096]{1,0:T(8,128)(2,1)} %param.2) | copy-start | bytes 1572868
  0.6 16.0 %collective-permute-start.11 = (bf16[64,4096]{1,0:T(8,128)(2,1)}, bf16[64,4096]{1,0:T(8,128)(2,1)S(1)}, u32[]{:S(2)}, u32[]{:S(2)}) collective-permute-start(bf16[64,4096]{1,0:T(8,128)(2,1)} %param.2), channel_id=1, source_target_pairs={{0,8},{1,9},{2,10},{3,11},{4,12},{5,13},{6,14},{7,15},{8,0},{9,1},... | collective-permute-start | bytes 1572872 | tf_op jit(solution)/shard_map/ppermute | solution.py:89
  3.7 8.3 %collective-permute-start = (bf16[64,4096]{1,0:T(8,128)(2,1)}, bf16[64,4096]{1,0:T(8,128)(2,1)S(1)}, u32[]{:S(2)}, u32[]{:S(2)}) collective-permute-start(bf16[64,4096]{1,0:T(8,128)(2,1)} %param.2), channel_id=1, source_target_pairs={{0,4},{1,5},{2,6},{3,7},{4,0},{5,1},{6,2},{7,3},{8,12},{9,13},{10,... | collective-permute-start | bytes 1572872 | tf_op jit(solution)/shard_map/ppermute | solution.py:89
  3.7 24.7 %collective-permute-start.15 = (bf16[64,4096]{1,0:T(8,128)(2,1)}, bf16[64,4096]{1,0:T(8,128)(2,1)S(1)}, u32[]{:S(2)}, u32[]{:S(2)}) collective-permute-start(bf16[64,4096]{1,0:T(8,128)(2,1)} %param.2), channel_id=1, source_target_pairs={{0,24},{1,25},{2,26},{3,27},{4,28},{5,29},{6,30},{7,31},{8,16},{9,... | collective-permute-start | bytes 1572872 | tf_op jit(solution)/shard_map/ppermute | solution.py:89
  5.2 27.7 %collective-permute-start.13 = (bf16[64,4096]{1,0:T(8,128)(2,1)}, bf16[64,4096]{1,0:T(8,128)(2,1)S(1)}, u32[]{:S(2)}, u32[]{:S(2)}) collective-permute-start(bf16[64,4096]{1,0:T(8,128)(2,1)} %param.2), channel_id=1, source_target_pairs={{0,16},{1,17},{2,18},{3,19},{4,20},{5,21},{6,22},{7,23},{8,24},{9,... | collective-permute-start | bytes 1572872 | tf_op jit(solution)/shard_map/ppermute | solution.py:89
  12.1 26.0 %copy-start.2 = (bf16[64,4096]{1,0:T(8,128)(2,1)S(1)}, bf16[64,4096]{1,0:T(8,128)(2,1)}, u32[]{:S(2)}) copy-start(bf16[64,4096]{1,0:T(8,128)(2,1)} %get-tuple-element.27) | copy-start | bytes 1572868
  12.1 31.9 %collective-permute-start.3 = (bf16[2048,128]{0,1:T(8,128)(2,1)S(1)}, bf16[2048,128]{0,1:T(8,128)(2,1)S(1)}, u32[]{:S(2)}, u32[]{:S(2)}) collective-permute-start(bf16[2048,128]{0,1:T(8,128)(2,1)S(1)} %bitcast.89), channel_id=1, source_target_pairs={{0,1},{1,0},{2,3},{3,2},{4,5},{5,4},{6,7},{7,6},{8,9},{9,8},{10,11... | collective-permute-start | bytes 1572872 | tf_op jit(solution)/shard_map/ppermute | solution.py:89
  14.2 29.8 %collective-permute-start.2 = (bf16[2048,128]{0,1:T(8,128)(2,1)S(1)}, bf16[2048,128]{0,1:T(8,128)(2,1)S(1)}, u32[]{:S(2)}, u32[]{:S(2)}) collective-permute-start(bf16[2048,128]{0,1:T(8,128)(2,1)S(1)} %bitcast.90), channel_id=1, source_target_pairs={{1,2},{2,1},{5,6},{6,5},{9,10},{10,9},{13,14},{14,13},{17,18},{18,... | collective-permute-start | bytes 1572872 | tf_op jit(solution)/shard_map/ppermute | solution.py:89
  16.7 16.3 %collective-permute-start.12 = (bf16[64,4096]{1,0:T(8,128)(2,1)S(1)}, bf16[64,4096]{1,0:T(8,128)(2,1)S(1)}, u32[]{:S(2)}, u32[]{:S(2)}) collective-permute-start(bf16[64,4096]{1,0:T(8,128)(2,1)S(1)} %collective-permute-done.11), channel_id=1, source_target_pairs={{0,4},{1,5},{2,6},{3,7},{4,0},{5,1},{6,2},{7,3},{8,12},{9,13},{10,... | collective-permute-start | bytes 1572872 | tf_op jit(solution)/shard_map/ppermute | solution.py:89
  28.4 15.3 %collective-permute-start.1 = (bf16[2048,128]{0,1:T(8,128)(2,1)S(1)}, bf16[2048,128]{0,1:T(8,128)(2,1)S(1)}, u32[]{:S(2)}, u32[]{:S(2)}) collective-permute-start(bf16[2048,128]{0,1:T(8,128)(2,1)S(1)} %bitcast.91), channel_id=1, source_target_pairs={{0,2},{3,1},{4,6},{7,5},{8,10},{11,9},{12,14},{15,13},{16,18},{19,... | collective-permute-start | bytes 1572872 | tf_op jit(solution)/shard_map/ppermute | solution.py:89
  32.9 4.4 %collective-permute-start.16 = (bf16[64,4096]{1,0:T(8,128)(2,1)S(1)}, bf16[64,4096]{1,0:T(8,128)(2,1)S(1)}, u32[]{:S(2)}, u32[]{:S(2)}) collective-permute-start(bf16[64,4096]{1,0:T(8,128)(2,1)S(1)} %collective-permute-done.15), channel_id=1, source_target_pairs={{0,4},{1,5},{2,6},{3,7},{4,0},{5,1},{6,2},{7,3},{8,12},{9,13},{10,... | collective-permute-start | bytes 1572872 | tf_op jit(solution)/shard_map/ppermute | solution.py:89
  33.0 2.6 %collective-permute-start.14 = (bf16[64,4096]{1,0:T(8,128)(2,1)S(1)}, bf16[64,4096]{1,0:T(8,128)(2,1)S(1)}, u32[]{:S(2)}, u32[]{:S(2)}) collective-permute-start(bf16[64,4096]{1,0:T(8,128)(2,1)S(1)} %collective-permute-done.13), channel_id=1, source_target_pairs={{0,4},{1,5},{2,6},{3,7},{4,0},{5,1},{6,2},{7,3},{8,12},{9,13},{10,... | collective-permute-start | bytes 1572872 | tf_op jit(solution)/shard_map/ppermute | solution.py:89
  41.9 5.6 %collective-permute-start.17 = (f32[64,512]{1,0:T(8,128)S(1)}, f32[64,512]{1,0:T(8,128)S(1)}, u32[]{:S(2)}, u32[]{:S(2)}) collective-permute-start(f32[64,512]{1,0:T(8,128)S(1)} %slice_add_fusion.3), channel_id=1, source_target_pairs={{0,1},{1,0},{2,3},{3,2},{4,5},{5,4},{6,7},{7,6},{8,9},{9,8},{10,11... | collective-permute-start | bytes 393224 | tf_op jit(solution)/shard_map/ppermute | solution.py:89
  44.1 14.8 %copy-start = (f32[4096,64]{0,1:T(8,128)S(1)}, f32[4096,64]{0,1:T(8,128)}, u32[]{:S(2)}) copy-start(f32[4096,64]{0,1:T(8,128)} %param.3) | copy-start | bytes 3145732
  47.5 8.5 %collective-permute-start.18 = (f32[64,512]{1,0:T(8,128)S(1)}, f32[64,512]{1,0:T(8,128)S(1)}, u32[]{:S(2)}, u32[]{:S(2)}) collective-permute-start(f32[64,512]{1,0:T(8,128)S(1)} %fusion.49), channel_id=1, source_target_pairs={{0,2},{1,3},{2,0},{3,1},{4,6},{5,7},{6,4},{7,5},{8,10},{9,11},{10,... | collective-permute-start | bytes 393224 | tf_op jit(solution)/shard_map/ppermute | solution.py:89
  63.1 5.0 %collective-permute-start.22 = (f32[64,512]{1,0:T(8,128)S(1)}, f32[64,512]{1,0:T(8,128)S(1)}, u32[]{:S(2)}, u32[]{:S(2)}) collective-permute-start(f32[64,512]{1,0:T(8,128)S(1)} %slice_add_fusion.2), channel_id=1, source_target_pairs={{0,1},{1,0},{2,3},{3,2},{4,5},{5,4},{6,7},{7,6},{8,9},{9,8},{10,11... | collective-permute-start | bytes 393224 | tf_op jit(solution)/shard_map/ppermute | solution.py:89
  63.7 45.7 %collective-permute-start.4 = (bf16[2048,128]{0,1:T(8,128)(2,1)S(1)}, bf16[2048,128]{0,1:T(8,128)(2,1)S(1)}, u32[]{:S(2)}, u32[]{:S(2)}) collective-permute-start(bf16[2048,128]{0,1:T(8,128)(2,1)S(1)} %get-tuple-element.14), channel_id=1, source_target_pairs={{1,24},{2,11},{5,28},{6,15},{9,16},{10,3},{13,20},{14,7}} | collective-permute-start | bytes 1572872 | tf_op jit(solution)/shard_map/ppermute | solution.py:89
  64.4 45.0 %collective-permute-start.10 = (bf16[2048,128]{0,1:T(8,128)(2,1)S(1)}, bf16[2048,128]{0,1:T(8,128)(2,1)S(1)}, u32[]{:S(2)}, u32[]{:S(2)}) collective-permute-start(bf16[2048,128]{0,1:T(8,128)(2,1)S(1)} %get-tuple-element.15), channel_id=1, source_target_pairs={{17,16},{18,3},{21,20},{22,7},{25,24},{26,11},{29,28},{30,15}} | collective-permute-start | bytes 1572872 | tf_op jit(solution)/shard_map/ppermute | solution.py:89
  65.1 44.3 %collective-permute-start.9 = (bf16[2048,128]{0,1:T(8,128)(2,1)S(1)}, bf16[2048,128]{0,1:T(8,128)(2,1)S(1)}, u32[]{:S(2)}, u32[]{:S(2)}) collective-permute-start(bf16[2048,128]{0,1:T(8,128)(2,1)S(1)} %get-tuple-element.16), channel_id=1, source_target_pairs={{17,24},{18,11},{21,28},{22,15},{25,16},{26,3},{29,20},{30,7}} | collective-permute-start | bytes 1572872 | tf_op jit(solution)/shard_map/ppermute | solution.py:89
  65.8 30.1 %collective-permute-start.7 = (bf16[2048,128]{0,1:T(8,128)(2,1)S(1)}, bf16[2048,128]{0,1:T(8,128)(2,1)S(1)}, u32[]{:S(2)}, u32[]{:S(2)}) collective-permute-start(bf16[2048,128]{0,1:T(8,128)(2,1)S(1)} %get-tuple-element.18), channel_id=1, source_target_pairs={{1,17},{2,18},{3,19},{5,21},{6,22},{7,23},{9,25},{10,26},{11,27},{... | collective-permute-start | bytes 1572872 | tf_op jit(solution)/shard_map/ppermute | solution.py:89
  68.1 11.9 %collective-permute-start.23 = (f32[64,512]{1,0:T(8,128)S(1)}, f32[64,512]{1,0:T(8,128)S(1)}, u32[]{:S(2)}, u32[]{:S(2)}) collective-permute-start(f32[64,512]{1,0:T(8,128)S(1)} %fusion.48), channel_id=1, source_target_pairs={{0,2},{1,3},{2,0},{3,1},{4,6},{5,7},{6,4},{7,5},{8,10},{9,11},{10,... | collective-permute-start | bytes 393224 | tf_op jit(solution)/shard_map/ppermute | solution.py:89
  80.0 14.3 %collective-permute-start.6 = (bf16[2048,128]{0,1:T(8,128)(2,1)S(1)}, bf16[2048,128]{0,1:T(8,128)(2,1)S(1)}, u32[]{:S(2)}, u32[]{:S(2)}) collective-permute-start(bf16[2048,128]{0,1:T(8,128)(2,1)S(1)} %get-tuple-element.19), channel_id=1, source_target_pairs={{0,8},{1,9},{2,10},{4,12},{5,13},{6,14},{8,0},{9,1},{10,2},{12,4},... | collective-permute-start | bytes 1572872 | tf_op jit(solution)/shard_map/ppermute | solution.py:89
  94.3 14.3 %collective-permute-start.8 = (bf16[2048,128]{0,1:T(8,128)(2,1)S(1)}, bf16[2048,128]{0,1:T(8,128)(2,1)S(1)}, u32[]{:S(2)}, u32[]{:S(2)}) collective-permute-start(bf16[2048,128]{0,1:T(8,128)(2,1)S(1)} %get-tuple-element.17), channel_id=1, source_target_pairs={{1,25},{2,26},{3,27},{5,29},{6,30},{7,31},{9,17},{10,18},{11,19},{... | collective-permute-start | bytes 1572872 | tf_op jit(solution)/shard_map/ppermute | solution.py:89
  95.9 13.6 %collective-permute-start.5 = (bf16[2048,128]{0,1:T(8,128)(2,1)S(1)}, bf16[2048,128]{0,1:T(8,128)(2,1)S(1)}, u32[]{:S(2)}, u32[]{:S(2)}) collective-permute-start(bf16[2048,128]{0,1:T(8,128)(2,1)S(1)} %get-tuple-element.21), channel_id=1, source_target_pairs={{1,16},{2,3},{5,20},{6,7},{9,24},{10,11},{13,28},{14,15}} | collective-permute-start | bytes 1572872 | tf_op jit(solution)/shard_map/ppermute | solution.py:89
  108.7 46.4 %collective-permute-start.21 = (f32[64,2048]{1,0:T(8,128)S(1)}, f32[64,2048]{1,0:T(8,128)S(1)}, u32[]{:S(2)}, u32[]{:S(2)}) collective-permute-start(f32[64,2048]{1,0:T(8,128)S(1)} %get-tuple-element.24), channel_id=1, source_target_pairs={{0,0},{1,8},{2,16},{3,24},{4,4},{5,12},{6,20},{7,28},{8,1},{9,9},{... | collective-permute-start | bytes 1572872 | tf_op jit(solution)/shard_map/ppermute | solution.py:89
  109.4 8.7 %collective-permute-start.19 = (f32[64,2048]{1,0:T(8,128)S(1)}, f32[64,2048]{1,0:T(8,128)S(1)}, u32[]{:S(2)}, u32[]{:S(2)}) collective-permute-start(f32[64,2048]{1,0:T(8,128)S(1)} %get-tuple-element.25), channel_id=1, source_target_pairs={{0,20},{1,21},{2,22},{3,23},{4,8},{5,9},{6,10},{7,11},{8,28},{9,29... | collective-permute-start | bytes 1572872 | tf_op jit(solution)/shard_map/ppermute | solution.py:89
  118.1 37.0 %collective-permute-start.20 = (f32[64,2048]{1,0:T(8,128)S(1)}, f32[64,2048]{1,0:T(8,128)S(1)}, u32[]{:S(2)}, u32[]{:S(2)}) collective-permute-start(f32[64,2048]{1,0:T(8,128)S(1)} %collective-permute-done.19), channel_id=1, source_target_pairs={{0,1},{1,9},{2,17},{3,25},{4,6},{5,14},{6,22},{7,30},{8,0},{9,8},{... | collective-permute-start | bytes 1572872 | tf_op jit(solution)/shard_map/ppermute | solution.py:89
